TPU v7x, 512 devices: a whole 4x8x8 slice. The times are simulated.
512 devices in a mesh: expert: 8 (over x, z_hi), tensor: 64 (over y, z_lo, core).
Axes of the slice: x: 4, y: 8, z: 8 (z_hi: 2, z_lo: 4; z = z_hi * 4 + z_lo), core: 2. Of those that a mesh axis runs over, the one named last changes fastest.
Arguments:
- tokens: bfloat16 [384, 6144], P('expert', 'tensor'), may hold values from -6 to 6
- expert_ids: int32 [384, 2], P('expert'), may hold values from 0 to 7, as said below
- route_weight: int32 [384, 2], P('expert'), may hold values from 1 to 4095
- gate_weight: bfloat16 [8, 6144, 8192], P('expert', None, 'tensor'), may hold values from -0.078125 to 0.078125
- up_weight: bfloat16 [8, 6144, 8192], P('expert', None, 'tensor'), may hold values from -0.078125 to 0.078125
- down_weight: bfloat16 [8, 8192, 6144], P('expert', 'tensor'), may hold values from -0.0625 to 0.0625
Outputs:
- mixed: bfloat16 [384, 6144], P('expert', 'tensor')
- expert_load: float32 [2, 8], replicated
Inputs may be any that keep to these rules, and one draw needn't show every extreme that they name: `expert_ids`: each row names two different experts. The hot expert is the one named in the first column of the first row of every aligned block of 48 rows (the tokens of one expert group), the same in all blocks. In each block exactly 42 rows name the hot expert, in either column; every other expert is named by 7 or 8 rows of each block, and by exactly 8 rows in some.
All inputs are finite; a program needn't handle non-finite values.
Results may differ from a plain program's by a relative error of at most 0.005.
Values may be sent and summed in bfloat16 or wider, within the bound.
A program may use at most 64 MiB of HBM per device.

v0:
```python
import jax
import jax.numpy as jnp
from jax import lax
from jax.sharding import PartitionSpec as P


def filled_up(lines, length):
    spare = -len(lines) % length
    return jnp.pad(lines, [(0, spare)] + [(0, 0)] * (lines.ndim - 1))


def from_root(value, axis, root):
    lines = jnp.where(lax.axis_index(axis) == root, value, jnp.zeros_like(value)).reshape(
        -1, *value.shape[1:][-1:]
    )
    padded = filled_up(lines, lax.axis_size(axis))
    own = lax.psum_scatter(padded, axis, scatter_dimension=0, tiled=True)
    return lax.all_gather(own, axis, axis=0, tiled=True)[: len(lines)].reshape(value.shape)


def gather_turned(arrays, axis, dims):
    turned = [jnp.moveaxis(a, dim, 0) for a, dim in zip(arrays, dims)]
    widths = [t[0].size for t in turned]
    both = jnp.concatenate([t.reshape(-1, w) for t, w in zip(turned, widths)], axis=1)
    out = lax.all_gather(both, axis, axis=0, tiled=True)
    blocks = jnp.split(out, [sum(widths[:k]) for k in range(1, len(widths))], axis=1)
    return tuple(
        (
            jnp.moveaxis(b.reshape(-1, *t.shape[1:]), 0, dim)
            for b, t, dim in zip(blocks, turned, dims)
        )
    )


def split_up(value, dim, length):
    lengths = value.shape
    blocks = value.reshape(*lengths[:dim], length, lengths[dim] // length, *lengths[dim + 1 :])
    return jnp.moveaxis(blocks, dim, 0)


def sum_at_owner(value, axis, dim):
    length = lax.axis_size(axis)
    blocks = lax.all_to_all(split_up(value, dim, length), axis, 0, 0, tiled=True)
    return jnp.sum(blocks, axis=0)


def from_everyone(value, axis):
    copies = jnp.broadcast_to(value, (lax.axis_size(axis), *value.shape))
    return lax.all_to_all(copies, axis, split_axis=0, concat_axis=0, tiled=True)


def of_everyone(value, axis):
    return from_everyone(value, axis).sum(axis=0)


def swiglu(gate_value, up_value):
    return (jax.nn.silu(gate_value) * up_value).astype(jnp.bfloat16)


def matmul(left, right):
    return jnp.dot(left, right, preferred_element_type=jnp.float32)


def route_stats(id_block, raw_block, labels):
    weights = raw_block.astype(jnp.float32)
    route_share = weights / jnp.sum(weights, axis=1, keepdims=True)
    flat_chosen = (
        (id_block[:, :, None] == labels[None, None, :])
        .astype(jnp.int32)
        .reshape(-1, labels.shape[0])
    )
    chosen_float = flat_chosen.astype(jnp.float32)
    stats = jnp.stack(
        [jnp.sum(chosen_float, axis=0), jnp.sum(route_share.reshape(-1, 1) * chosen_float, axis=0)]
    )
    return (route_share, flat_chosen, stats)


def local(tokens, expert_ids, route_weight, gate_weight, up_weight, down_weight):
    tok_rows = expert_ids.shape[0]
    experts = lax.axis_size("expert") * gate_weight.shape[0]
    hot_rows = tok_rows - tok_rows // 8 * min(experts - 2, 1)
    capacity = (2 * tok_rows - hot_rows + experts - 2) // (experts - 1)
    hot_id = expert_ids[0, 0]
    own_gate = gate_weight[0]
    own_up = up_weight[0]
    own_down = down_weight[0]
    hot_gate_w, hot_up_w, hot_down_w = (
        from_root(own_gate, "expert", hot_id),
        from_root(own_up, "expert", hot_id),
        from_root(own_down, "expert", hot_id),
    )
    labels = jnp.arange(experts, dtype=jnp.int32)
    route_share, flat_chosen, local_stats = route_stats(expert_ids, route_weight, labels)
    cold_chosen = flat_chosen * (labels != hot_id).astype(jnp.int32)[None, :]
    slot_index = jnp.sum((jnp.cumsum(cold_chosen, axis=0) - 1) * cold_chosen, axis=1)
    is_live = jnp.sum(cold_chosen, axis=1)
    target = jnp.sum(cold_chosen * labels[None, :], axis=1) * capacity + slot_index
    buffer_rows = jnp.arange(experts * capacity, dtype=jnp.int32)
    cold_pick = ((target[None, :] == buffer_rows[:, None]) & (is_live[None, :] == 1)).astype(
        jnp.bfloat16
    )
    cold_pick = jnp.sum(cold_pick.reshape(experts * capacity, tok_rows, 2), axis=2)
    hot_match = (expert_ids == hot_id).astype(jnp.int32)
    hot_flag = jnp.sum(hot_match, axis=1)
    hot_rank = jnp.cumsum(hot_flag) - 1
    hot_slots = jnp.arange(hot_rows, dtype=jnp.int32)
    hot_pick = ((hot_rank[None, :] == hot_slots[:, None]) & (hot_flag[None, :] == 1)).astype(
        jnp.bfloat16
    )
    feature_width = tokens.shape[1]
    cold_send = (
        matmul(cold_pick, tokens).astype(jnp.bfloat16).reshape(experts, capacity, feature_width)
    )
    cold_recv = lax.all_to_all(
        cold_send, "expert", split_axis=0, concat_axis=0, tiled=True
    ).reshape(experts * capacity, feature_width)
    hot_input = matmul(hot_pick, tokens).astype(jnp.bfloat16)
    cold_piece, hot_piece = gather_turned((cold_recv, hot_input), "tensor", (1, 1))
    cold_gate = matmul(cold_piece, own_gate)
    cold_up = matmul(cold_piece, own_up)
    hot_gate = matmul(hot_piece, hot_gate_w)
    hot_up = matmul(hot_piece, hot_up_w)
    cold_part = matmul(swiglu(cold_gate, cold_up), own_down)
    hot_part = matmul(swiglu(hot_gate, hot_up), hot_down_w)
    model_width = cold_part.shape[1]
    returned = lax.all_to_all(
        cold_part.reshape(experts, capacity, model_width),
        "expert",
        split_axis=0,
        concat_axis=0,
        tiled=True,
    ).reshape(experts * capacity, model_width)
    assign_weight = route_share.reshape(2 * tok_rows) * is_live.astype(jnp.float32)
    cold_out = jnp.sum(
        (returned[target] * assign_weight[:, None]).reshape(tok_rows, 2, model_width), axis=1
    )
    hot_weight = jnp.sum(route_share * hot_match.astype(jnp.float32), axis=1)
    hot_out = hot_part[jnp.clip(hot_rank, 0, hot_rows - 1)] * hot_weight[:, None]
    mixed = sum_at_owner(cold_out + hot_out, "tensor", 1).astype(jnp.bfloat16)
    expert_load = of_everyone(local_stats, "expert") / tok_rows
    return (mixed, expert_load)


def solution(mesh):
    placed = (
        P("expert", "tensor"),
        P("expert", None),
        P("expert", None),
        P("expert", None, "tensor"),
        P("expert", None, "tensor"),
        P("expert", "tensor", None),
    )
    return jax.shard_map(
        local, mesh=mesh, in_specs=placed, out_specs=(P("expert", "tensor"), P()), check_vma=False
    )
```

profile of v0, /device:TPU:1, one launch (start us, length us, event | category | flops | bytes accessed | tf_op | source)
XLA Modules:
  0.0 469.7 jit_solution(4374038837522308300)
XLA Ops:
  9.9 2.7 bitcast_select_fusion.2
  12.6 1.3 copy-done.4
  14.0 1.3 bitcast_select_fusion
  18.6 13.3 %all-to-all-start = ((bf16[8,8,96]{2,1,0:T(8,128)(2,1)}), bf16[8,8,96]{2,1,0:T(8,128)(2,1)S(1)}, u32[]{:S(2)}, u32[]{:S(2)}) async-start(bf16[8,8,96]{2,1,0:T(8,128)(2,1)} %fusion.28), calls=%async_computation | async-start | bytes 32768 | tf_op jit(solution)/shard_map/all_to_all | solution.py:115
  33.0 7.8 %all-to-all-done = bf16[8,8,96]{2,1,0:T(8,128)(2,1)S(1)} async-done(((bf16[8,8,96]{2,1,0:T(8,128)(2,1)}), bf16[8,8,96]{2,1,0:T(8,128)(2,1)S(1)}, u32[]{:S(2)}, u32[]{:S(2)}) %all-to-all-start) | async-done | bytes 12320 | tf_op jit(solution)/shard_map/all_to_all | solution.py:115
  43.0 72.0 %reduce-scatter.4.cloned.1.call-done = bf16[768,128]{1,0:T(8,128)(2,1)} async-done(((bf16[6144,128]{1,0:T(8,128)(2,1)}), bf16[768,128]{1,0:T(8,128)(2,1)}) %reduce-scatter.4.cloned.1.call-update) | async-done | bytes 196624 | tf_op jit(solution)/shard_map/reduce_scatter | solution.py:17
  115.1 98.7 %reduce-scatter.8.cloned.1.call-done = bf16[16,6144]{1,0:T(8,128)(2,1)} async-done(((bf16[128,6144]{1,0:T(8,128)(2,1)}), bf16[16,6144]{1,0:T(8,128)(2,1)}) %reduce-scatter.8.cloned.1.call-update) | async-done | bytes 196624 | tf_op jit(solution)/shard_map/reduce_scatter | solution.py:17
  213.8 2.1 fusion.4
  215.9 4.0 fusion
  219.9 3.7 all-to-all-start.1
  223.7 107.7 %reduce-scatter.6.cloned.1.call-done = bf16[768,128]{1,0:T(8,128)(2,1)} async-done(((bf16[6144,128]{1,0:T(8,128)(2,1)}), bf16[768,128]{1,0:T(8,128)(2,1)}) %reduce-scatter.6.cloned.1.call-update) | async-done | bytes 196624 | tf_op jit(solution)/shard_map/reduce_scatter | solution.py:17
  333.4 3.6 all-to-all-start.3
  337.0 2.7 gather_fusion
  339.7 3.8 gather.11
  343.5 5.1 %multiply_reduce_fusion = f32[48,6144]{1,0:T(8,128)S(1)} fusion(f32[48,2,6144]{2,1,0:T(2,128)} %gather.11, f32[48,2]{1,0:T(8,128)S(1)} %copy.64), kind=kLoop, calls=%fused_computation.2 | loop fusion | flops 884736 | bytes 3539328 | tf_op jit(solution)/shard_map/reduce_sum | solution.py:135
  348.6 1.8 reduce_sum.120
  350.4 2.4 fusion.8
  352.9 49.2 %all-gather.9.cloned.1.call-done = bf16[6144,128]{1,0:T(8,128)(2,1)} async-done(((bf16[768,128]{1,0:T(8,128)(2,1)}), bf16[6144,128]{1,0:T(8,128)(2,1)}) %all-gather.9.cloned.1.call-update) | async-done | bytes 1572880 | tf_op jit(solution)/shard_map/all_gather | solution.py:18
  402.1 3.2 fusion.36
  405.3 1.9 gather_fusion.1
  407.3 2.0 gather.13
  409.5 2.1 copy.65
  411.6 10.4 %all-to-all-start.2 = ((f32[64,48,96]{2,1,0:T(8,128)}), f32[64,48,96]{2,1,0:T(8,128)S(1)}, u32[]{:S(2)}, u32[]{:S(2)}) async-start(f32[64,48,96]{2,1,0:T(8,128)} %copy.65), calls=%async_computation.5 | async-start | bytes 3145728 | tf_op jit(solution)/shard_map/all_to_all | solution.py:43
  422.5 39.1 %all-to-all-done.2 = f32[64,48,96]{2,1,0:T(8,128)S(1)} async-done(((f32[64,48,96]{2,1,0:T(8,128)}), f32[64,48,96]{2,1,0:T(8,128)S(1)}, u32[]{:S(2)}, u32[]{:S(2)}) %all-to-all-start.2) | async-done | bytes 1179680 | tf_op jit(solution)/shard_map/all_to_all | solution.py:43
  (76 shorter events, 11.5 us)
Async XLA Ops:
  8.0 9.8 %copy-start = (bf16[48,96]{1,0:T(8,128)(2,1)S(1)}, bf16[48,96]{1,0:T(8,128)(2,1)}, u32[]{:S(2)}) copy-start(bf16[48,96]{1,0:T(8,128)(2,1)} %param.6) | copy-start | bytes 27652
  8.0 107.0 %reduce-scatter.4.cloned.1.call-start = ((), (), s32[]{:S(2)}) async-start(), calls=%async_computation.8 | async-start | bytes 1769472 | tf_op jit(solution)/shard_map/reduce_scatter | solution.py:17
  12.6 1.4 copy-start.4
  12.6 201.1 %reduce-scatter.8.cloned.1.call-start = ((), (), s32[]{:S(2)}) async-start(), calls=%async_computation.12 | async-start | bytes 1769472 | tf_op jit(solution)/shard_map/reduce_scatter | solution.py:17
  15.3 0.7 copy-start.6
  15.3 26.4 %copy-start.5 = (bf16[1,6144,128]{2,1,0:T(8,128)(2,1)S(1)}, bf16[1,6144,128]{2,1,0:T(8,128)(2,1)}, u32[]{:S(2)}) copy-start(bf16[1,6144,128]{2,1,0:T(8,128)(2,1)} %param.10) | copy-start | bytes 4718596
  18.6 22.3 %all-to-all-start = ((bf16[8,8,96]{2,1,0:T(8,128)(2,1)}), bf16[8,8,96]{2,1,0:T(8,128)(2,1)S(1)}, u32[]{:S(2)}, u32[]{:S(2)}) async-start(bf16[8,8,96]{2,1,0:T(8,128)(2,1)} %fusion.28), calls=%async_computation | async-start | bytes 32768 | tf_op jit(solution)/shard_map/all_to_all | solution.py:115
  31.9 181.9 %all-gather.5.cloned.1.call-start = ((), (), s32[]{:S(2)}) async-start(), calls=%async_computation.7 | async-start | bytes 1597440 | tf_op jit(solution)/shard_map/all_gather | solution.py:25
  41.6 289.8 %reduce-scatter.6.cloned.1.call-start = ((), (), s32[]{:S(2)}) async-start(), calls=%async_computation.10 | async-start | bytes 1769472 | tf_op jit(solution)/shard_map/reduce_scatter | solution.py:17
  42.9 170.9 %copy-start.3 = (bf16[1,6144,128]{2,1,0:T(8,128)(2,1)S(1)}, bf16[1,6144,128]{2,1,0:T(8,128)(2,1)}, u32[]{:S(2)}) copy-start(bf16[1,6144,128]{2,1,0:T(8,128)(2,1)} %param.9) | copy-start | bytes 4718596
  43.0 307.5 %all-gather.7.cloned.1.call-start = ((), (), s32[]{:S(2)}) async-start(), calls=%async_computation.9 | async-start | bytes 1769472 | tf_op jit(solution)/shard_map/all_gather | solution.py:18
  115.0 237.9 %all-gather.11.cloned.1.call-start = ((), (), s32[]{:S(2)}) async-start(), calls=%async_computation.13 | async-start | bytes 1769472 | tf_op jit(solution)/shard_map/all_gather | solution.py:18
  213.8 2.1 copy-start.1
  219.9 111.7 %copy-start.7 = (s32[48,2]{0,1:T(2,128)S(1)}, s32[48,2]{0,1:T(2,128)}, u32[]{:S(2)}) copy-start(s32[48,2]{0,1:T(2,128)} %param.8) | copy-start | bytes 1156
  219.9 112.9 %all-to-all-start.1 = ((f32[8,8,6144]{2,1,0:T(8,128)}), f32[8,8,6144]{2,1,0:T(8,128)S(1)}, u32[]{:S(2)}, u32[]{:S(2)}) async-start(f32[8,8,6144]{2,1,0:T(8,128)} %fusion), calls=%async_computation.1 | async-start | bytes 3145728 | tf_op jit(solution)/shard_map/all_to_all | solution.py:127
  223.7 178.5 %all-gather.9.cloned.1.call-start = ((), (), s32[]{:S(2)}) async-start(), calls=%async_computation.11 | async-start | bytes 1769472 | tf_op jit(solution)/shard_map/all_gather | solution.py:18
  333.4 78.1 %all-to-all-start.3 = ((f32[8,2,8]{2,1,0:T(2,128)}), f32[8,2,8]{2,1,0:T(2,128)S(1)}, u32[]{:S(2)}, u32[]{:S(2)}) async-start(f32[8,2,8]{2,1,0:T(2,128)} %broadcast_in_dim.5), calls=%async_computation.6 | async-start | bytes 16384 | tf_op jit(solution)/shard_map/all_to_all | solution.py:49
  407.3 2.0 copy-start.2
  411.6 50.0 %all-to-all-start.2 = ((f32[64,48,96]{2,1,0:T(8,128)}), f32[64,48,96]{2,1,0:T(8,128)S(1)}, u32[]{:S(2)}, u32[]{:S(2)}) async-start(f32[64,48,96]{2,1,0:T(8,128)} %copy.65), calls=%async_computation.5 | async-start | bytes 3145728 | tf_op jit(solution)/shard_map/all_to_all | solution.py:43
Sparse Core Ops, SparseCore 0:
  13.4 101.5 reduce-scatter.3
  119.6 94.0 reduce-scatter.7
  218.4 113.0 reduce-scatter.5
Sparse Core Ops, SparseCore 1:
  41.7 119.9 all-gather.4
  164.7 75.4 all-gather.6
  243.3 80.9 all-gather.10
  331.5 70.5 all-gather.8
where the time goes:
time: 470 us
  waiting for transfers between devices  375 us (80%)
  starting transfers between devices  31.2 us (7%)
  local copies, waits for them, and re-layouts  20 us (4%)
  between operations  16.4 us (3%)
  other arithmetic  14.8 us (3%)
  matrix products  12.6 us (3%)
    reduce_scatter x3, waiting for transfers between devices, from_root(): own = lax.psum_scatter(padded, axis, scatter_dimension=0, tiled=True)  278 us
    all_gather x3, waiting for transfers between devices, from_root(): lax.all_gather(own, axis, axis=0, tiled=True)[:len(lines)]  49.3 us
    all_to_all x1, waiting for transfers between devices, sum_at_owner(): lax.all_to_all(split_up(value, dim, length), axis, 0, 0, tiled=True)  39.1 us
    all_to_all x1, starting transfers between devices, local(): lax.all_to_all(cold_send, 'expert', split_axis=0, concat_axis=0, tiled=True)  13.3 us
    dot_general x6, matrix products, matmul(): return jnp.dot(left, right, preferred_element_type=jnp.float32)  12.6 us
    all_to_all x1, starting transfers between devices, sum_at_owner(): lax.all_to_all(split_up(value, dim, length), axis, 0, 0, tiled=True)  10.4 us
  transfers between devices with their start and end apart: 11, of which 6 were waited for; matrix products, arithmetic and copies ran while one was open for 9% of the time, Pallas kernels for 0%

commit v1 on v0

--- a/solution.py
+++ b/solution.py
@@ -15,7 +15,9 @@
     )
     padded = filled_up(lines, lax.axis_size(axis))
     own = lax.psum_scatter(padded, axis, scatter_dimension=0, tiled=True)
-    return lax.all_gather(own, axis, axis=0, tiled=True)[: len(lines)].reshape(value.shape)
+    return jnp.concatenate(
+        lax.all_to_all(jnp.stack([own] * lax.axis_size(axis)), axis, 0, 0), axis=0
+    )[: len(lines)].reshape(value.shape)
 
 
 def gather_turned(arrays, axis, dims):

time: 470 us -> 532 us (1.13)
  starting transfers between devices: 31.2 us -> 60.1 us
  waiting for transfers between devices: 375 us -> 398 us
    all_gather x1, waiting for transfers between devices: 0.02 us -> 114 us  [gather_turned(): out = lax.all_gather(both, axis, axis=0, tiled=True)]
    reduce_scatter x3, waiting for transfers between devices: 278 us -> 197 us  [from_root(): own = lax.psum_scatter(padded, axis, scatter_dimension=0, tiled=True)]
    all_gather x3 -> x0, waiting for transfers between devices: 49.3 us -> none  [from_root(): lax.all_gather(own, axis, axis=0, tiled=True)[:len(lines)]]
    all_to_all x1, waiting for transfers between devices: 0.01 us -> 28.4 us  [local(): lax.all_to_all(cold_part.reshape(experts, capacity, model_width), 'expert...]
    all_to_all x0 -> x3, starting transfers between devices: none -> 13 us  [from_root(): lax.all_to_all(jnp.stack([own] * lax.axis_size(axis)), axis, 0, 0)]
    all_to_all x0 -> x3, waiting for transfers between devices: none -> 12.8 us  [from_root(): lax.all_to_all(jnp.stack([own] * lax.axis_size(axis)), axis, 0, 0)]
    all_to_all x1, starting transfers between devices: 10.4 us -> 21.4 us  [sum_at_owner(): lax.all_to_all(split_up(value, dim, length), axis, 0, 0, tiled=True)]
    another operation x0 -> x3, local copies, waits for them, and re-layouts: none -> 6.8 us  [from_root(): jnp.stack([own] * lax.axis_size(axis))]
  transfers between devices with their start and end apart: 11 -> 11, of which waited for: 6 -> 7; matrix products, arithmetic and copies ran while one was open for 9% -> 9% of each run, Pallas kernels for 0% -> 0%
where the time goes in v1:
time: 532 us; the launch traced here: 531 us
  waiting for transfers between devices  398 us (75%)
  starting transfers between devices  60.1 us (11%)
  local copies, waits for them, and re-layouts  25.3 us (5%)
  other arithmetic  18.1 us (3%)
  between operations  16.5 us (3%)
  matrix products  12.6 us (2%)
    reduce_scatter x3, waiting for transfers between devices, from_root(): own = lax.psum_scatter(padded, axis, scatter_dimension=0, tiled=True)  197 us
    all_gather x1, waiting for transfers between devices, gather_turned(): out = lax.all_gather(both, axis, axis=0, tiled=True)  114 us
    all_to_all x1, waiting for transfers between devices, sum_at_owner(): lax.all_to_all(split_up(value, dim, length), axis, 0, 0, tiled=True)  39.1 us
    all_to_all x1, waiting for transfers between devices, local(): lax.all_to_all(cold_part.reshape(experts, capacity, model_width), 'expert...  28.4 us
    all_to_all x1, starting transfers between devices, sum_at_owner(): lax.all_to_all(split_up(value, dim, length), axis, 0, 0, tiled=True)  21.4 us
    all_to_all x1, starting transfers between devices, local(): lax.all_to_all(cold_send, 'expert', split_axis=0, concat_axis=0, tiled=True)  13.3 us
    all_to_all x3, starting transfers between devices, from_root(): lax.all_to_all(jnp.stack([own] * lax.axis_size(axis)), axis, 0, 0)  13 us
    all_to_all x3, waiting for transfers between devices, from_root(): lax.all_to_all(jnp.stack([own] * lax.axis_size(axis)), axis, 0, 0)  12.8 us
  transfers between devices with their start and end apart: 11, of which 7 were waited for; matrix products, arithmetic and copies ran while one was open for 9% of the time, Pallas kernels for 0%

profile of v1, /device:TPU:1, one launch (start us, length us, event | category | flops | bytes accessed | tf_op | source)
XLA Modules:
  0.0 530.9 jit_solution(833503414291721951)
XLA Ops:
  12.5 13.3 %all-to-all-start = ((bf16[8,8,96]{2,1,0:T(8,128)(2,1)}), bf16[8,8,96]{2,1,0:T(8,128)(2,1)S(1)}, u32[]{:S(2)}, u32[]{:S(2)}) async-start(bf16[8,8,96]{2,1,0:T(8,128)(2,1)} %fusion.28), calls=%async_computation | async-start | bytes 32768 | tf_op jit(solution)/shard_map/all_to_all | solution.py:117
  27.6 7.2 %all-to-all-done = bf16[8,8,96]{2,1,0:T(8,128)(2,1)S(1)} async-done(((bf16[8,8,96]{2,1,0:T(8,128)(2,1)}), bf16[8,8,96]{2,1,0:T(8,128)(2,1)S(1)}, u32[]{:S(2)}, u32[]{:S(2)}) %all-to-all-start) | async-done | bytes 12320 | tf_op jit(solution)/shard_map/all_to_all | solution.py:117
  36.2 2.7 bitcast_select_fusion.2
  38.9 114.0 %all-gather.2.cloned.1.call-done = bf16[6144,106]{1,0:T(8,128)(2,1)} async-done(((bf16[96,106]{1,0:T(8,128)(2,1)}), bf16[6144,106]{1,0:T(8,128)(2,1)}) %all-gather.2.cloned.1.call-update) | async-done | bytes 1302544 | tf_op jit(solution)/shard_map/all_gather | solution.py:27
  155.1 3.9 fusion
  159.0 8.7 %all-to-all-start.1 = ((f32[8,8,6144]{2,1,0:T(8,128)}), f32[8,8,6144]{2,1,0:T(8,128)S(1)}, u32[]{:S(2)}, u32[]{:S(2)}) async-start(f32[8,8,6144]{2,1,0:T(8,128)} %fusion), calls=%async_computation.1 | async-start | bytes 3145728 | tf_op jit(solution)/shard_map/all_to_all | solution.py:129
  167.8 2.7 bitcast_select_fusion.1
  170.5 28.4 %all-to-all-done.1 = f32[8,8,6144]{2,1,0:T(8,128)S(1)} async-done(((f32[8,8,6144]{2,1,0:T(8,128)}), f32[8,8,6144]{2,1,0:T(8,128)S(1)}, u32[]{:S(2)}, u32[]{:S(2)}) %all-to-all-start.1) | async-done | bytes 1572896 | tf_op jit(solution)/shard_map/all_to_all | solution.py:129
  201.2 4.3 all-to-all-start.2
  205.6 2.7 bitcast_select_fusion
  208.2 97.3 %reduce-scatter.6.cloned.1.call-done = bf16[768,128]{1,0:T(8,128)(2,1)} async-done(((bf16[6144,128]{1,0:T(8,128)(2,1)}), bf16[768,128]{1,0:T(8,128)(2,1)}) %reduce-scatter.6.cloned.1.call-update) | async-done | bytes 196624 | tf_op jit(solution)/shard_map/reduce_scatter | solution.py:17
  305.6 2.3 stack.13
  307.9 4.3 all-to-all-start.3
  312.2 99.3 %reduce-scatter.8.cloned.1.call-done = bf16[16,6144]{1,0:T(8,128)(2,1)} async-done(((bf16[128,6144]{1,0:T(8,128)(2,1)}), bf16[16,6144]{1,0:T(8,128)(2,1)}) %reduce-scatter.8.cloned.1.call-update) | async-done | bytes 196624 | tf_op jit(solution)/shard_map/reduce_scatter | solution.py:17
  413.8 4.4 all-to-all-start.4
  419.6 2.7 gather_fusion
  422.3 3.7 gather.11
  425.9 5.0 multiply_reduce_fusion
  432.7 2.4 fusion.8
  435.2 12.8 %all-to-all-done.4 = bf16[8,16,6144]{2,1,0:T(8,128)(2,1)} async-done(((bf16[8,16,6144]{2,1,0:T(8,128)(2,1)}), bf16[8,16,6144]{2,1,0:T(8,128)(2,1)}, u32[]{:S(2)}, u32[]{:S(2)}) %all-to-all-start.4) | async-done | bytes 1572896 | tf_op jit(solution)/shard_map/all_to_all | solution.py:19
  448.6 3.5 all-to-all-start.6
  452.1 3.2 fusion.36
  461.6 21.4 %all-to-all-start.5 = ((f32[64,48,96]{2,1,0:T(8,128)}), f32[64,48,96]{2,1,0:T(8,128)S(1)}, u32[]{:S(2)}, u32[]{:S(2)}) async-start(f32[64,48,96]{2,1,0:T(8,128)} %copy.65), calls=%async_computation.8 | async-start | bytes 3145728 | tf_op jit(solution)/shard_map/all_to_all | solution.py:45
  483.6 39.1 %all-to-all-done.5 = f32[64,48,96]{2,1,0:T(8,128)S(1)} async-done(((f32[64,48,96]{2,1,0:T(8,128)}), f32[64,48,96]{2,1,0:T(8,128)S(1)}, u32[]{:S(2)}, u32[]{:S(2)}) %all-to-all-start.5) | async-done | bytes 1179680 | tf_op jit(solution)/shard_map/all_to_all | solution.py:45
  (72 shorter events, 25.1 us)
Async XLA Ops:
  8.0 3.8 copy-start
  12.5 22.3 %all-to-all-start = ((bf16[8,8,96]{2,1,0:T(8,128)(2,1)}), bf16[8,8,96]{2,1,0:T(8,128)(2,1)S(1)}, u32[]{:S(2)}, u32[]{:S(2)}) async-start(bf16[8,8,96]{2,1,0:T(8,128)(2,1)} %fusion.28), calls=%async_computation | async-start | bytes 32768 | tf_op jit(solution)/shard_map/all_to_all | solution.py:117
  25.8 127.1 %all-gather.2.cloned.1.call-start = ((), (), s32[]{:S(2)}) async-start(), calls=%async_computation.10 | async-start | bytes 1597440 | tf_op jit(solution)/shard_map/all_gather | solution.py:27
  35.5 135.0 %reduce-scatter.4.cloned.1.call-start = ((), (), s32[]{:S(2)}) async-start(), calls=%async_computation.11 | async-start | bytes 1769472 | tf_op jit(solution)/shard_map/reduce_scatter | solution.py:17
  38.9 114.0 %copy-start.3 = (bf16[1,6144,128]{2,1,0:T(8,128)(2,1)S(1)}, bf16[1,6144,128]{2,1,0:T(8,128)(2,1)}, u32[]{:S(2)}) copy-start(bf16[1,6144,128]{2,1,0:T(8,128)(2,1)} %param.9) | copy-start | bytes 4718596
  152.9 2.1 copy-start.1
  159.0 39.9 %all-to-all-start.1 = ((f32[8,8,6144]{2,1,0:T(8,128)}), f32[8,8,6144]{2,1,0:T(8,128)S(1)}, u32[]{:S(2)}, u32[]{:S(2)}) async-start(f32[8,8,6144]{2,1,0:T(8,128)} %fusion), calls=%async_computation.1 | async-start | bytes 3145728 | tf_op jit(solution)/shard_map/all_to_all | solution.py:129
  167.7 137.8 %reduce-scatter.6.cloned.1.call-start = ((), (), s32[]{:S(2)}) async-start(), calls=%async_computation.12 | async-start | bytes 1769472 | tf_op jit(solution)/shard_map/reduce_scatter | solution.py:17
  201.2 104.4 %all-to-all-start.2 = ((bf16[8,768,128]{2,1,0:T(8,128)(2,1)}), bf16[8,768,128]{2,1,0:T(8,128)(2,1)}, u32[]{:S(2)}, u32[]{:S(2)}) async-start(bf16[8,768,128]{2,1,0:T(8,128)(2,1)} %stack.12), calls=%async_computation.3 | async-start | bytes 3145728 | tf_op jit(solution)/shard_map/all_to_all | solution.py:19
  205.5 206.0 %reduce-scatter.8.cloned.1.call-start = ((), (), s32[]{:S(2)}) async-start(), calls=%async_computation.13 | async-start | bytes 1769472 | tf_op jit(solution)/shard_map/reduce_scatter | solution.py:17
  307.9 103.6 %all-to-all-start.3 = ((bf16[8,768,128]{2,1,0:T(8,128)(2,1)}), bf16[8,768,128]{2,1,0:T(8,128)(2,1)}, u32[]{:S(2)}, u32[]{:S(2)}) async-start(bf16[8,768,128]{2,1,0:T(8,128)(2,1)} %stack.13), calls=%async_computation.5 | async-start | bytes 3145728 | tf_op jit(solution)/shard_map/all_to_all | solution.py:19
  413.8 4.6 copy-start.5
  413.8 4.7 copy-start.4
  413.8 34.2 %all-to-all-start.4 = ((bf16[8,16,6144]{2,1,0:T(8,128)(2,1)}), bf16[8,16,6144]{2,1,0:T(8,128)(2,1)}, u32[]{:S(2)}, u32[]{:S(2)}) async-start(bf16[8,16,6144]{2,1,0:T(8,128)(2,1)} %stack.14), calls=%async_computation.7 | async-start | bytes 3145728 | tf_op jit(solution)/shard_map/all_to_all | solution.py:19
  448.6 13.0 %all-to-all-start.6 = ((f32[8,2,8]{2,1,0:T(2,128)}), f32[8,2,8]{2,1,0:T(2,128)S(1)}, u32[]{:S(2)}, u32[]{:S(2)}) async-start(f32[8,2,8]{2,1,0:T(2,128)} %broadcast_in_dim.5), calls=%async_computation.9 | async-start | bytes 16384 | tf_op jit(solution)/shard_map/all_to_all | solution.py:51
  457.2 2.0 copy-start.2
  461.6 61.0 %all-to-all-start.5 = ((f32[64,48,96]{2,1,0:T(8,128)}), f32[64,48,96]{2,1,0:T(8,128)S(1)}, u32[]{:S(2)}, u32[]{:S(2)}) async-start(f32[64,48,96]{2,1,0:T(8,128)} %copy.65), calls=%async_computation.8 | async-start | bytes 3145728 | tf_op jit(solution)/shard_map/all_to_all | solution.py:45
Sparse Core Ops, SparseCore 0:
  35.7 117.2 all-gather.1
Sparse Core Ops, SparseCore 1:
  40.6 94.1 reduce-scatter.3
  172.8 132.7 reduce-scatter.5
  310.1 101.4 reduce-scatter.7
